TPU v7x, 64 devices: a 2x2x8 block of a 4x4x8 slice. The times are simulated.
64 devices in a mesh: batch: 4 (over x, y), dap: 16 (over z, core).
Axes of the slice: x: 2, y: 2, z: 8, core: 2. Of those that a mesh axis runs over, the one named last changes fastest.
The devices are a block of a 4x4x8 slice.
Arguments:
- z_pair: bfloat16 [1536, 384, 128], P(('batch', 'dap')), parts along dimension 0
- pair_mask: int32 [1536, 384], P(('batch', 'dap')), parts along dimension 0
- dz_out: bfloat16 [1536, 384, 128], P(('batch', 'dap')), parts along dimension 0
- ln_in_scale: bfloat16 [128], replicated
- ln_in_offset: bfloat16 [128], replicated
- w_in: bfloat16 [128, 512], replicated
- b_in: bfloat16 [512], replicated
- ln_out_scale: bfloat16 [128], replicated
- ln_out_offset: bfloat16 [128], replicated
- w_out: bfloat16 [128, 128], replicated
- b_out: bfloat16 [128], replicated
- w_gate: bfloat16 [128, 128], replicated
- b_gate: bfloat16 [128], replicated
Outputs:
- output 1: bfloat16 [1536, 384, 128], P(('batch', 'dap')), parts along dimension 0
- output 2: bfloat16 [512], P('batch'), parts along dimension 0
- output 3: bfloat16 [512], P('batch'), parts along dimension 0
- output 4: bfloat16 [512, 512], P('batch'), parts along dimension 0
- output 5: bfloat16 [2048], P('batch'), parts along dimension 0
- output 6: bfloat16 [512], P('batch'), parts along dimension 0
- output 7: bfloat16 [512], P('batch'), parts along dimension 0
- output 8: bfloat16 [512, 128], P('batch'), parts along dimension 0
- output 9: bfloat16 [512], P('batch'), parts along dimension 0
- output 10: bfloat16 [512, 128], P('batch'), parts along dimension 0
- output 11: bfloat16 [512], P('batch'), parts along dimension 0
There are 4 independent parts. A program takes and returns all parts, laid end to end along the dimension named above; an argument that names none is the same for every part.
All inputs are finite; a program needn't handle non-finite values.
Results may differ from a plain program's by a relative error of at most 0.0194336.
Values are sent between devices in bfloat16 or wider.
A program may use at most 768 MiB of HBM per device.

v0:
```python
import jax
import jax.numpy as jnp
from jax import lax
from jax.sharding import PartitionSpec as P

LN_EPS = 1e-5


def norm_forward(x_val, ln_scale, ln_offset, axis_id):
    mean_val = jnp.mean(x_val, axis=axis_id, keepdims=True)
    centered = x_val - mean_val
    inv_std = lax.rsqrt(jnp.mean(centered * centered, axis=axis_id, keepdims=True) + LN_EPS)
    x_hat = centered * inv_std
    return x_hat, inv_std, x_hat * ln_scale + ln_offset


def norm_backward(grad_out, x_hat, inv_std, ln_scale, axis_id):
    grad_hat = grad_out * ln_scale
    mean_grad = jnp.mean(grad_hat, axis=axis_id, keepdims=True)
    mean_proj = jnp.mean(grad_hat * x_hat, axis=axis_id, keepdims=True)
    return inv_std * (grad_hat - mean_grad - x_hat * mean_proj)


def input_side(z_part, mask_part, ln_in_scale, ln_in_offset, w_in, b_in):
    hidden = w_in.shape[1] // 4
    in_hat, in_inv, in_aff = norm_forward(z_part.astype(jnp.float32), ln_in_scale.astype(jnp.float32), ln_in_offset.astype(jnp.float32), -1)
    z_norm = in_aff.astype(jnp.bfloat16)
    proj_t = jnp.einsum('de,rnd->ern', w_in, z_norm, preferred_element_type=jnp.float32) + b_in.astype(jnp.float32)[:, None, None]
    proj_a = proj_t[:hidden]
    proj_b = proj_t[hidden:2 * hidden]
    sig_a = jax.nn.sigmoid(proj_t[2 * hidden:3 * hidden])
    sig_b = jax.nn.sigmoid(proj_t[3 * hidden:])
    mask_f = mask_part.astype(jnp.float32)[None]
    act_a = (mask_f * sig_a * proj_a).astype(jnp.bfloat16)
    act_b = (mask_f * sig_b * proj_b).astype(jnp.bfloat16)
    return in_hat, in_inv, z_norm, proj_a, proj_b, sig_a, sig_b, mask_f, act_a, act_b


def output_chain(tri_out, gate_lin, dy_part, ln_out_scale, ln_out_offset, w_out, b_out):
    out_scale = ln_out_scale.astype(jnp.float32)[:, None, None]
    out_offset = ln_out_offset.astype(jnp.float32)[:, None, None]
    out_hat, out_inv, out_aff = norm_forward(tri_out, out_scale, out_offset, 0)
    o_norm = out_aff.astype(jnp.bfloat16)
    update = (jnp.einsum('crn,cd->rnd', o_norm, w_out, preferred_element_type=jnp.float32) + b_out.astype(jnp.float32)).astype(jnp.bfloat16)
    sig_g = jax.nn.sigmoid(gate_lin)
    dy_f = dy_part.astype(jnp.float32)
    d_update = (sig_g * dy_f).astype(jnp.bfloat16)
    d_gate_lin = dy_f * update.astype(jnp.float32) * sig_g * (1.0 - sig_g)
    d_onorm = jnp.einsum('cd,rnd->crn', w_out, d_update, preferred_element_type=jnp.float32).astype(jnp.bfloat16).astype(jnp.float32)
    d_tri = norm_backward(d_onorm, out_hat, out_inv, out_scale, 0).astype(jnp.bfloat16)
    return d_tri, o_norm, out_hat, d_onorm, d_update, d_gate_lin


def input_backward(d_act_a, d_act_b, proj_a, proj_b, sig_a, sig_b, mask_f, z_norm, in_hat, in_inv, dy_part, d_gate_lin, ln_in_scale, w_in, w_gate):
    grad_a = d_act_a.astype(jnp.bfloat16).astype(jnp.float32) * mask_f
    grad_b = d_act_b.astype(jnp.bfloat16).astype(jnp.float32) * mask_f
    d_proj = jnp.concatenate([grad_a * sig_a, grad_b * sig_b, grad_a * proj_a * sig_a * (1.0 - sig_a), grad_b * proj_b * sig_b * (1.0 - sig_b)], axis=0)
    d_b_in = jnp.sum(d_proj, axis=(1, 2))
    d_b_gate = jnp.sum(d_gate_lin, axis=(0, 1))
    proj_grad16 = d_proj.astype(jnp.bfloat16)
    gate_grad16 = d_gate_lin.astype(jnp.bfloat16)
    d_w_in = jnp.einsum('rnd,ern->de', z_norm, proj_grad16, preferred_element_type=jnp.float32)
    d_w_gate = jnp.einsum('rnd,rne->de', z_norm, gate_grad16, preferred_element_type=jnp.float32)
    d_znorm = (jnp.einsum('ern,de->rnd', proj_grad16, w_in, preferred_element_type=jnp.float32) + jnp.einsum('rne,de->rnd', gate_grad16, w_gate, preferred_element_type=jnp.float32)).astype(jnp.bfloat16).astype(jnp.float32)
    d_in_scale = jnp.sum(d_znorm * in_hat, axis=(0, 1))
    d_in_offset = jnp.sum(d_znorm, axis=(0, 1))
    d_z = (dy_part.astype(jnp.float32) + norm_backward(d_znorm, in_hat, in_inv, ln_in_scale.astype(jnp.float32), -1)).astype(jnp.bfloat16)
    return d_z, d_in_scale, d_in_offset, d_w_in, d_b_in, d_w_gate, d_b_gate


def local_grads(z_loc, mask_loc, dy_loc, ln_in_scale, ln_in_offset, w_in, b_in, ln_out_scale, ln_out_offset, w_out, b_out, w_gate, b_gate):
    in_hat, in_inv, z_norm, proj_a, proj_b, sig_a, sig_b, mask_f, act_a, act_b = input_side(z_loc, mask_loc, ln_in_scale, ln_in_offset, w_in, b_in)
    gate_lin = jnp.einsum('rnd,de->rne', z_norm, w_gate, preferred_element_type=jnp.float32) + b_gate.astype(jnp.float32)
    b_full = lax.all_gather(act_b, 'dap', axis=1, tiled=True)
    tri_out = jnp.einsum('cik,cjk->cij', act_a, b_full, preferred_element_type=jnp.float32)
    d_tri, o_norm, out_hat, d_onorm, d_update, d_gate_lin = output_chain(tri_out, gate_lin, dy_loc, ln_out_scale, ln_out_offset, w_out, b_out)
    d_w_out = jnp.einsum('crn,rnd->cd', o_norm, d_update, preferred_element_type=jnp.float32)
    d_b_out = jnp.sum(d_update.astype(jnp.float32), axis=(0, 1))
    d_out_scale = jnp.sum(d_onorm * out_hat, axis=(1, 2))
    d_out_offset = jnp.sum(d_onorm, axis=(1, 2))
    d_act_a = jnp.einsum('cij,cjk->cik', d_tri, b_full, preferred_element_type=jnp.float32)
    d_b_part = jnp.einsum('cij,cik->cjk', d_tri, act_a, preferred_element_type=jnp.float32)
    d_act_b = lax.psum_scatter(d_b_part, 'dap', scatter_dimension=1, tiled=True)
    d_z, d_in_scale, d_in_offset, d_w_in, d_b_in, d_w_gate, d_b_gate = input_backward(d_act_a, d_act_b, proj_a, proj_b, sig_a, sig_b, mask_f, z_norm, in_hat, in_inv, dy_loc, d_gate_lin, ln_in_scale, w_in, w_gate)
    summed = lax.psum((d_in_scale, d_in_offset, d_w_in, d_b_in, d_out_scale, d_out_offset, d_w_out, d_b_out, d_w_gate, d_b_gate), 'dap')
    return (d_z,) + tuple(grad_piece.astype(jnp.bfloat16) for grad_piece in summed)


def solution(mesh):
    pair_spec = P(('batch', 'dap'), None, None)
    mask_spec = P(('batch', 'dap'), None)
    vec_rep = P(None)
    mat_rep = P(None, None)
    vec_part = P('batch')
    mat_part = P('batch', None)
    in_specs = (pair_spec, mask_spec, pair_spec, vec_rep, vec_rep, mat_rep, vec_rep, vec_rep, vec_rep, mat_rep, vec_rep, mat_rep, vec_rep)
    out_specs = (pair_spec, vec_part, vec_part, mat_part, vec_part, vec_part, vec_part, mat_part, vec_part, mat_part, vec_part)
    return jax.shard_map(local_grads, mesh=mesh, in_specs=in_specs, out_specs=out_specs, check_vma=False)
```

profile of v0, /device:TPU:21, one launch (start us, length us, event | category | flops | bytes accessed | tf_op | source)
XLA Modules:
  0.0 862.5 jit_solution(9562915352008641829)
XLA Ops:
  12.6 4.1 fusion.22
  19.4 5.7 multiply_convert_fusion
  27.3 4.3 copy.36
  31.8 9.4 %convert_reduce_fusion.3 = (f32[128]{0:T(128)}, bf16[24,384,128]{2,1,0:T(8,128)(2,1)S(1)}, f32[24,384,128]{2,1,0:T(8,128)}) fusion(bf16[24,384,128]{2,1,0:T(8,128)(2,1)} %param.15, f32[128]{0:T(128)S(1)} %convert_element_type.135, bf16[128,128]{1,0:T(8,128)(2,1)S(1)} %copy-done.17, bf16[24,384,128]{2,1,0:T(8,128)(2,1)S(1)} %copy-done.3, ...), kind=kOutput, calls=%fused_computation.54 | convolution fusion | flops 319684480 | bytes 11905024 | tf_op jit(solution)/shard_map/rnd,de->rne/dot_general | solution.py:73
  44.9 4.6 copy.39
  49.5 4.5 copy.37
  54.0 173.7 %all-gather.2.cloned.1.call-done = bf16[128,384,384]{2,0,1:T(8,128)(2,1)} async-done(((bf16[128,24,384]{2,0,1:T(8,128)(2,1)}), bf16[128,384,384]{2,0,1:T(8,128)(2,1)}) %all-gather.2.cloned.1.call-update) | async-done | bytes 37748752 | tf_op jit(solution)/shard_map/all_gather | solution.py:74
  227.6 38.9 %fusion.69 = (f32[24,384]{1,0:T(8,128)S(1)}, f32[128,24,384]{2,1,0:T(8,128)}) fusion(bf16[128,24,384]{2,1,0:T(8,128)(2,1)} %copy.37, bf16[128,384,384]{2,0,1:T(8,128)(2,1)} %all-gather.2.cloned.1.call-done), kind=kOutput, calls=%fused_computation.94 | convolution fusion | flops 907140096 | bytes 44863488 | tf_op jit(solution)/shard_map/cik,cjk->cij/dot_general | solution.py:75
  266.6 3.0 multiply_reduce_fusion
  270.3 6.2 fusion.27
  276.5 2.8 fusion.25
  279.3 29.1 %fusion.71 = f32[128,384,384]{2,1,0:T(8,128)} fusion(bf16[128,24,384]{2,1,0:T(8,128)(2,1)} %fusion.25, bf16[128,24,384]{2,1,0:T(8,128)(2,1)} %copy.37), kind=kOutput, calls=%fused_computation.96 | convolution fusion | flops 905969664 | bytes 80216064 | tf_op jit(solution)/shard_map/cij,cik->cjk/dot_general | solution.py:82
  308.4 73.0 %copy.43 = f32[128,384,384]{0,2,1:T(8,128)} copy(f32[128,384,384]{2,1,0:T(8,128)} %fusion.71) | data formatting | bytes 150994944 | tf_op jit(solution)/shard_map/cij,cik->cjk/dot_general | solution.py:82
  384.8 5.5 fusion.70
  391.8 3.3 fusion.48
  395.1 60.2 %fusion = bf16[128,24,384]{2,1,0:T(8,128)(2,1)} fusion(bf16[128,24,384]{2,1,0:T(8,128)(2,1)S(1)} %copy-done.5, bf16[128,384,384]{2,0,1:T(8,128)(2,1)} %all-gather.2.cloned.1.call-done), kind=kOutput, calls=%fused_computation | convolution fusion | flops 905969664 | bytes 42467328 | tf_op jit(solution)/shard_map/cij,cjk->cik/dot_general | solution.py:81
  455.3 4.5 copy.41
  459.8 311.7 %reduce-scatter.2.cloned.1.call-done = f32[128,24,384]{0,2,1:T(8,128)} async-done(((f32[128,384,384]{0,2,1:T(8,128)}), f32[128,24,384]{0,2,1:T(8,128)}) %reduce-scatter.2.cloned.1.call-update) | async-done | bytes 4718608 | tf_op jit(solution)/shard_map/reduce_scatter | solution.py:83
  771.5 10.0 %fusion.41 = (f32[128,24,384]{0,2,1:T(8,128)S(1)}, f32[128,24,384]{0,2,1:T(8,128)S(1)}, f32[128,24,384]{0,2,1:T(8,128)S(1)}, f32[128,24,384]{0,2,1:T(8,128)S(1)}) fusion(f32[24,384]{1,0:T(8,128)S(1)} %copy-done.13, bf16[128,24,384]{0,2,1:T(8,128)(2,1)} %copy.41, f32[512,24,384]{0,2,1:T(8,128)} %copy-done.1, f32[128,24,384]{0,2,1:T(8,128)} %reduce-scatter.2.cloned.1.call-done), kind=kLoop, calls=%fused_computation.63 | loop fusion | flops 24772608 | bytes 44863488 | tf_op jit(solution)/shard_map/mul | solution.py:57
  782.9 3.7 convolution_bitcast_fusion
  786.6 4.4 fusion.54
  791.0 8.2 fusion.33
  799.3 7.3 fusion.32
  806.6 48.9 %all-reduce.2 = (bf16[128]{0:T(256)(128)(2,1)}, bf16[128]{0:T(256)(128)(2,1)}, bf16[128,512]{1,0:T(8,128)(2,1)}, bf16[512]{0:T(512)(128)(2,1)}, bf16[128]{0:T(25...) all-reduce(f32[128]{0:T(128)S(1)} %get-tuple-element.13, ...), channel_id=1, replica_groups=mesh['batch'=4,'dap'=16] {'dap'}, use_global_device_ids=true, to_apply=%region_10.0 | all-reduce | flops 99584 | bytes 597504 | tf_op jit(solution)/shard_map/psum | solution.py:85
  (71 shorter events, 20.9 us)
Async XLA Ops:
  7.2 9.5 %copy-start = (bf16[128,512]{1,0:T(8,128)(2,1)S(1)}, bf16[128,512]{1,0:T(8,128)(2,1)}, u32[]{:S(2)}) copy-start(bf16[128,512]{1,0:T(8,128)(2,1)} %param.18) | copy-start | bytes 393220
  7.2 9.5 %copy-start.3 = (bf16[24,384,128]{2,1,0:T(8,128)(2,1)S(1)}, bf16[24,384,128]{2,1,0:T(8,128)(2,1)}, u32[]{:S(2)}) copy-start(bf16[24,384,128]{2,1,0:T(8,128)(2,1)} %param.13) | copy-start | bytes 7077892
  7.2 220.4 %all-gather.2.cloned.1.call-start = ((), (), s32[]{:S(2)}) async-start(), calls=%async_computation.1 | async-start | bytes 40108032 | tf_op jit(solution)/shard_map/all_gather | solution.py:74
  10.2 9.2 %copy-start.12 = (f32[24,384]{1,0:T(8,128)}, f32[24,384]{1,0:T(8,128)S(1)}, u32[]{:S(2)}) copy-start(f32[24,384]{1,0:T(8,128)S(1)} %convert_element_type.128) | copy-start | bytes 110596
  19.4 7.9 copy-start.1
  27.3 4.5 copy-start.19
  27.3 4.5 copy-start.20
  27.3 4.5 copy-start.21
  27.3 4.5 copy-start.17
  31.7 739.8 %reduce-scatter.2.cloned.1.call-start = ((), (), s32[]{:S(2)}) async-start(), calls=%async_computation.2 | async-start | bytes 80216064 | tf_op jit(solution)/shard_map/reduce_scatter | solution.py:83
  31.8 11.0 %copy-start.14 = (bf16[128,128]{1,0:T(8,128)(2,1)S(1)}, bf16[128,128]{1,0:T(8,128)(2,1)}, u32[]{:S(2)}) copy-start(bf16[128,128]{1,0:T(8,128)(2,1)} %param.22) | copy-start | bytes 98308
  41.2 1.5 copy-start.8
  266.6 3.8 copy-start.2
  270.3 6.2 copy-start.4
  384.8 5.5 copy-start.6
  384.8 5.5 copy-start.9
  390.3 1.4 copy-start.10
  391.1 4.0 copy-start.5
  455.3 316.2 %copy-start.13 = (f32[24,384]{1,0:T(8,128)S(1)}, f32[24,384]{1,0:T(8,128)}, u32[]{:S(2)}) copy-start(f32[24,384]{1,0:T(8,128)} %copy-done.12) | copy-start | bytes 110596
  786.6 4.4 copy-start.11
  786.6 4.4 copy-start.18
  791.0 8.3 copy-start.7
  799.3 7.3 copy-start.15
  799.3 7.3 copy-start.16
  (1 other events, 0.7 us)
Sparse Core Ops, SparseCore 0:
  31.8 195.7 all-gather.1
  381.6 389.8 reduce-scatter.1
where the time goes:
time: 872 us; the launch traced here: 863 us
  waiting for transfers between devices  485 us (56%)
  matrix products  168 us (19%)
  local copies, waits for them, and re-layouts  96.5 us (11%)
  blocking collectives  48.9 us (6%)
  other arithmetic  48.5 us (6%)
  between operations  14.6 us (2%)
    reduce_scatter x1, waiting for transfers between devices, local_grads(): d_act_b = lax.psum_scatter(d_b_part, 'dap', scatter_dimension=1, tiled=True)  312 us
    all_gather x1, waiting for transfers between devices, local_grads(): b_full = lax.all_gather(act_b, 'dap', axis=1, tiled=True)  174 us
    dot_general x1, local copies, waits for them, and re-layouts, local_grads(): jnp.einsum('cij,cik->cjk', d_tri, act_a, preferred_element_type=jnp.float32)  73 us
    dot_general x1, matrix products, local_grads(): jnp.einsum('cij,cjk->cik', d_tri, b_full, preferred_element_type=jnp.floa...  60.2 us
    psum x1, blocking collectives, local_grads(): lax.psum((d_in_scale, d_in_offset, d_w_in, d_b_in, d_out_scale, d_out_off...  48.9 us
    dot_general x1, matrix products, local_grads(): jnp.einsum('cik,cjk->cij', act_a, b_full, preferred_element_type=jnp.floa...  38.9 us
    dot_general x1, matrix products, local_grads(): jnp.einsum('cij,cik->cjk', d_tri, act_a, preferred_element_type=jnp.float32)  29.1 us
  transfers between devices with their start and end apart: 2, of which 2 were waited for; matrix products, arithmetic and copies ran while one was open for 11% of the time, Pallas kernels for 0%

commit v1 on v0

v1 whole, which is shorter than its diff:
```python
import functools
import jax
import jax.numpy as jnp
from jax import lax
from jax.experimental import pallas as pl
from jax.experimental.pallas import tpu as pltpu
from jax.sharding import PartitionSpec as P

LN_EPS = 1e-5
CHUNK = 8
F32 = jnp.float32
BF16 = jnp.bfloat16


def mm(x_val, y_val):
    return lax.dot_general(x_val, y_val, (((1,), (0,)), ((), ())), preferred_element_type=F32)


def mm_nt(x_val, y_val):
    return lax.dot_general(x_val, y_val, (((1,), (1,)), ((), ())), preferred_element_type=F32)


def mm_tn(x_val, y_val):
    return lax.dot_general(x_val, y_val, (((0,), (0,)), ((), ())), preferred_element_type=F32)


def norm_stats(x_val):
    size = x_val.shape[0]
    mean_val = jnp.sum(x_val, axis=0, keepdims=True) * (1.0 / size)
    centered = x_val - mean_val
    inv_std = lax.rsqrt(jnp.sum(centered * centered, axis=0, keepdims=True) * (1.0 / size) + LN_EPS)
    return centered * inv_std, inv_std


def norm_back(grad_hat, x_hat, inv_std):
    size = x_hat.shape[0]
    mean_grad = jnp.sum(grad_hat, axis=0, keepdims=True) * (1.0 / size)
    mean_proj = jnp.sum(grad_hat * x_hat, axis=0, keepdims=True) * (1.0 / size)
    return inv_std * (grad_hat - mean_grad - x_hat * mean_proj)


def lane_fold(x_val):
    total = x_val[:, :128]
    for tile in range(1, x_val.shape[1] // 128):
        total = total + x_val[:, tile * 128:(tile + 1) * 128]
    return total


def kernel(n_dev, z_ref, dy_ref, mask_ref, w_in_ref, w_gate_ref, w_out_ref, par_ref,
           dz_ref, gw_in_ref, gw_gate_ref, gw_out_ref, gvec_ref,
           w_in_t, w_gate_t, w_out_t, eye, cols,
           a_send, b_send, a_ch, b_ch, o_ch, o_row, do_send, do_ch, da_ch, da_row, db_ch, db_row,
           stage_a, stage_b, zn_keep, gg_keep, m_acc, v_acc, v_row, m_recv, v_recv, g_send, g_all,
           send_sem, a_sem, b_sem, o_sem, do_sem, da_sem, db_sem, m_sem, v_sem, g_sem):
    rows, num, chan = z_ref.shape
    n_chunk = rows // CHUNK
    part = chan // n_dev
    me = lax.axis_index('dap')
    shard = m_recv.shape[1]

    barrier = pltpu.get_barrier_semaphore()

    def ring_peer(step):
        half = step // 2 + 1
        offset = half + lax.rem(step, 2) * (n_dev - 2 * half)
        return lax.rem(me + offset, n_dev)

    def hello(step, carry):
        pl.semaphore_signal(barrier, inc=1, device_id={'dap': ring_peer(step)}, device_id_type=pl.DeviceIdType.MESH)
        return carry

    lax.fori_loop(0, n_dev - 1, hello, 0)

    row_id = lax.broadcasted_iota(jnp.int32, (chan, chan), 0)
    col_id = lax.broadcasted_iota(jnp.int32, (chan, chan), 1)
    eye[...] = jnp.where(row_id == col_id, 1.0, 0.0).astype(BF16)
    cols[...] = jnp.transpose(par_ref[...])
    for blk in range(4):
        w_in_t[blk * chan:(blk + 1) * chan, :] = jnp.transpose(w_in_ref[:, blk * chan:(blk + 1) * chan].astype(F32)).astype(BF16)
    w_gate_t[...] = jnp.transpose(w_gate_ref[...].astype(F32)).astype(BF16)
    w_out_t[...] = jnp.transpose(w_out_ref[...].astype(F32)).astype(BF16)
    m_acc[...] = jnp.zeros_like(m_acc)
    v_acc[...] = jnp.zeros_like(v_acc)

    def col(idx):
        return cols[:, idx:idx + 1]

    def exchange(src_of, dst_ref, send_idx, recv_sem):
        def one(step, carry):
            peer = ring_peer(step)
            pltpu.make_async_remote_copy(
                src_ref=src_of(peer), dst_ref=dst_ref, send_sem=send_sem.at[send_idx], recv_sem=recv_sem,
                device_id={'dap': peer}, device_id_type=pl.DeviceIdType.MESH).start()
            return carry
        lax.fori_loop(0, n_dev - 1, one, 0)
        pltpu.make_async_copy(src_of(me), dst_ref, recv_sem).start()

    def take(ref, sem):
        pltpu.make_async_copy(ref, ref, sem).wait()

    tiles = num // 128

    def get_row(stage, row):
        return jnp.concatenate([stage[tile, pl.ds(row, chan, stride=CHUNK), :] for tile in range(tiles)], axis=1)

    def put_row(stage, row, value):
        for tile in range(tiles):
            stage[tile, pl.ds(row, chan, stride=CHUNK), :] = value[:, tile * 128:(tile + 1) * 128]

    def spread(stage, block):
        for tile in range(tiles):
            stage[tile] = block[:, :, tile * 128:(tile + 1) * 128].astype(F32).reshape(chan * CHUNK, 128)

    def gather16(stage, dst):
        for tile in range(tiles):
            dst[:, :, tile * 128:(tile + 1) * 128] = stage[tile].reshape(chan, CHUNK, 128).astype(BF16)

    def input_norm(row):
        z_t = mm_nt(eye[...], z_ref[row])
        return norm_stats(z_t)

    def project(zn_t):
        def piece(blk):
            return mm(w_in_t[blk * chan:(blk + 1) * chan, :], zn_t) + col(blk)
        return piece(0), piece(1), jax.nn.sigmoid(piece(2)), jax.nn.sigmoid(piece(3))

    def mask_of(row):
        return mask_ref[pl.ds(row, 1), :].astype(F32)

    def input_chunk(chunk, carry):
        def one_row(r_in, carry_row):
            row = chunk * CHUNK + r_in
            in_hat, _ = input_norm(row)
            zn_t = (in_hat * col(5) + col(6)).astype(BF16)
            zn_keep[row] = zn_t
            proj_a, proj_b, sig_a, sig_b = project(zn_t)
            mask_f = mask_of(row)
            put_row(stage_a, r_in, mask_f * sig_a * proj_a)
            put_row(stage_b, r_in, mask_f * sig_b * proj_b)
            return carry_row
        lax.fori_loop(0, CHUNK, one_row, 0)
        gather16(stage_b, b_send.at[chunk])
        gather16(stage_a, a_send.at[chunk])

        @pl.when(chunk == 0)
        def _():
            pl.semaphore_wait(barrier, n_dev - 1)

        exchange(lambda peer: b_send.at[chunk, pl.ds(peer * part, part)],
                 b_ch.at[:, pl.ds(me * rows + chunk * CHUNK, CHUNK), :], 0, b_sem)
        exchange(lambda peer: a_send.at[chunk, pl.ds(peer * part, part)],
                 a_ch.at[chunk, :, pl.ds(me * CHUNK, CHUNK), :], 1, a_sem.at[chunk])
        return carry

    lax.fori_loop(0, n_chunk, input_chunk, 0)

    take(b_ch, b_sem)

    def tri_chunk(chunk, carry):
        take(a_ch.at[chunk], a_sem.at[chunk])

        def one(idx, carry_ch):
            o_ch[chunk, idx] = mm_nt(a_ch[chunk, idx], b_ch[idx])
            return carry_ch
        lax.fori_loop(0, part, one, 0)
        exchange(lambda peer: o_ch.at[chunk, :, pl.ds(peer * CHUNK, CHUNK), :],
                 o_row.at[chunk, pl.ds(me * part, part)], 2, o_sem.at[chunk])
        return carry

    lax.fori_loop(0, n_chunk, tri_chunk, 0)

    def chain_chunk(chunk, carry):
        take(o_row.at[chunk], o_sem.at[chunk])
        spread(stage_b, o_row.at[chunk])

        def one_row(r_in, carry_row):
            row = chunk * CHUNK + r_in
            out_hat, out_inv = norm_stats(get_row(stage_b, r_in))
            o_norm = (out_hat * col(7) + col(8)).astype(BF16)
            update = (mm(w_out_t[...], o_norm) + col(9)).astype(BF16).astype(F32)
            zn_t = zn_keep[row]
            sig_g = jax.nn.sigmoid(mm(w_gate_t[...], zn_t) + col(4))
            dy_t = mm_nt(eye[...], dy_ref[row])
            d_update = (sig_g * dy_t).astype(BF16)
            d_gate = dy_t * update * sig_g * (1.0 - sig_g)
            gate16 = d_gate.astype(BF16)
            gg_keep[row] = gate16
            v_acc[4] += lane_fold(d_gate)
            v_acc[9] += lane_fold(d_update.astype(F32))
            m_acc[4 * chan:(4 + 1) * chan, :] += mm_nt(zn_t, gate16)
            m_acc[5 * chan:(5 + 1) * chan, :] += mm_nt(o_norm, d_update)
            d_onorm = mm(w_out_ref[...], d_update).astype(BF16).astype(F32)
            v_acc[7] += lane_fold(d_onorm * out_hat)
            v_acc[8] += lane_fold(d_onorm)
            put_row(stage_a, r_in, norm_back(d_onorm * col(7), out_hat, out_inv))
            return carry_row
        lax.fori_loop(0, CHUNK, one_row, 0)
        gather16(stage_a, do_send.at[chunk])
        exchange(lambda peer: do_send.at[chunk, pl.ds(peer * part, part)],
                 do_ch.at[chunk, :, pl.ds(me * CHUNK, CHUNK), :], 3, do_sem.at[chunk])
        return carry

    lax.fori_loop(0, n_chunk, chain_chunk, 0)

    def da_chunk(chunk, carry):
        take(do_ch.at[chunk], do_sem.at[chunk])

        def one(idx, carry_ch):
            da_ch[chunk, idx] = mm(do_ch[chunk, idx], b_ch[idx]).astype(BF16)
            return carry_ch
        lax.fori_loop(0, part, one, 0)
        exchange(lambda peer: da_ch.at[chunk, :, pl.ds(peer * CHUNK, CHUNK), :],
                 da_row.at[chunk, pl.ds(me * part, part)], 4, da_sem.at[chunk])
        return carry

    lax.fori_loop(0, n_chunk, da_chunk, 0)

    def db_one(idx, carry):
        total = mm_tn(do_ch[0, idx], a_ch[0, idx])
        for chunk in range(1, n_chunk):
            total += mm_tn(do_ch[chunk, idx], a_ch[chunk, idx])
        db_ch[idx] = total.astype(BF16)
        return carry

    lax.fori_loop(0, part, db_one, 0)

    def db_chunk(chunk, carry):
        exchange(lambda peer: db_ch.at[:, pl.ds(peer * rows + chunk * CHUNK, CHUNK), :],
                 db_row.at[chunk, pl.ds(me * part, part)], 5, db_sem.at[chunk])
        return carry

    lax.fori_loop(0, n_chunk, db_chunk, 0)

    def back_chunk(chunk, carry):
        take(da_row.at[chunk], da_sem.at[chunk])
        take(db_row.at[chunk], db_sem.at[chunk])
        spread(stage_a, da_row.at[chunk])
        spread(stage_b, db_row.at[chunk])

        def one_row(r_in, carry_row):
            row = chunk * CHUNK + r_in
            mask_f = mask_of(row)
            zn_t = zn_keep[row]
            proj_a, proj_b, sig_a, sig_b = project(zn_t)
            grad_a = get_row(stage_a, r_in) * mask_f
            grad_b = get_row(stage_b, r_in) * mask_f
            d_znorm = mm(w_gate_ref[...], gg_keep[row])
            pieces = (grad_a * sig_a, grad_b * sig_b,
                      grad_a * proj_a * sig_a * (1.0 - sig_a), grad_b * proj_b * sig_b * (1.0 - sig_b))
            for blk in range(4):
                v_acc[blk] += lane_fold(pieces[blk])
                piece16 = pieces[blk].astype(BF16)
                m_acc[blk * chan:(blk + 1) * chan, :] += mm_nt(zn_t, piece16)
                d_znorm += mm(w_in_ref[:, blk * chan:(blk + 1) * chan], piece16)
            d_znorm = d_znorm.astype(BF16).astype(F32)
            in_hat, in_inv = input_norm(row)
            v_acc[5] += lane_fold(d_znorm * in_hat)
            v_acc[6] += lane_fold(d_znorm)
            dz_t = mm_nt(eye[...], dy_ref[row]) + norm_back(d_znorm * col(5), in_hat, in_inv)
            dz_ref[row] = jnp.transpose(dz_t).astype(BF16)
            return carry_row
        lax.fori_loop(0, CHUNK, one_row, 0)
        return carry

    lax.fori_loop(0, n_chunk, back_chunk, 0)

    v_row[...] = jnp.zeros_like(v_row)
    for idx in range(10):
        v_row[idx:idx + 1, :] = jnp.sum(jnp.transpose(v_acc[idx]), axis=0, keepdims=True)
    exchange(lambda peer: m_acc.at[pl.ds(peer * shard, shard)], m_recv.at[me], 6, m_sem)
    exchange(lambda peer: v_row, v_recv.at[me], 7, v_sem)
    take(m_recv, m_sem)
    g_send[...] = jnp.sum(m_recv[...], axis=0).astype(BF16)
    exchange(lambda peer: g_send, g_all.at[pl.ds(me * shard, shard)], 8, g_sem)
    take(v_recv, v_sem)
    gvec_ref[...] = jnp.sum(v_recv[...], axis=0).astype(BF16)
    take(g_all, g_sem)
    for blk in range(4):
        gw_in_ref[:, blk * chan:(blk + 1) * chan] = g_all[blk * chan:(blk + 1) * chan, :]
    gw_gate_ref[...] = g_all[4 * chan:5 * chan, :]
    gw_out_ref[...] = g_all[5 * chan:6 * chan, :]

    others = (n_dev - 1) * part
    for sent, ref in ((0, b_send), (1, a_send), (3, do_send), (2, o_row), (4, da_row), (5, db_row)):
        take(ref.at[:, pl.ds(0, others)], send_sem.at[sent])
    take(m_recv.at[pl.ds(0, n_dev - 1)], send_sem.at[6])
    take(v_recv.at[pl.ds(0, n_dev - 1)], send_sem.at[7])
    take(g_all.at[pl.ds(0, (n_dev - 1) * shard)], send_sem.at[8])


def local_grads(n_dev, z_loc, mask_loc, dy_loc, ln_in_scale, ln_in_offset, w_in, b_in, ln_out_scale, ln_out_offset, w_out, b_out, w_gate, b_gate):
    rows, num, chan = z_loc.shape
    n_chunk = rows // CHUNK
    part = chan // n_dev
    shard = 6 * chan // n_dev
    vecs = jnp.concatenate([b_in, b_gate, ln_in_scale, ln_in_offset, ln_out_scale, ln_out_offset, b_out]).astype(F32).reshape(10, chan)
    vecs = jnp.pad(vecs, ((0, chan - 10), (0, 0)))
    vmem = pl.BlockSpec(memory_space=pltpu.VMEM)
    shapes = [jax.ShapeDtypeStruct((rows, num, chan), BF16), jax.ShapeDtypeStruct((chan, 4 * chan), BF16),
              jax.ShapeDtypeStruct((chan, chan), BF16), jax.ShapeDtypeStruct((chan, chan), BF16), jax.ShapeDtypeStruct((16, chan), BF16)]
    by_row = pltpu.VMEM((n_chunk, chan, CHUNK, num), BF16)
    by_chan = pltpu.VMEM((n_chunk, part, n_dev * CHUNK, num), BF16)
    by_chan_all = pltpu.VMEM((part, num, num), BF16)
    stage = pltpu.VMEM((num // 128, chan * CHUNK, 128), F32)
    keep = pltpu.VMEM((rows, chan, num), BF16)
    scratch = [
        pltpu.VMEM((4 * chan, chan), BF16), pltpu.VMEM((chan, chan), BF16), pltpu.VMEM((chan, chan), BF16), pltpu.VMEM((chan, chan), BF16),
        pltpu.VMEM((chan, chan), F32),
        by_row, by_row, by_chan, by_chan_all,
        pltpu.VMEM((n_chunk, part, n_dev * CHUNK, num), F32), pltpu.VMEM((n_chunk, chan, CHUNK, num), F32),
        by_row, by_chan, by_chan, by_row, by_chan_all, by_row,
        stage, stage, keep, keep,
        pltpu.VMEM((6 * chan, chan), F32), pltpu.VMEM((10, chan, chan), F32), pltpu.VMEM((16, chan), F32),
        pltpu.VMEM((n_dev, shard, chan), F32), pltpu.VMEM((n_dev, 16, chan), F32),
        pltpu.VMEM((shard, chan), BF16), pltpu.VMEM((6 * chan, chan), BF16),
        pltpu.SemaphoreType.DMA((9,)),
        pltpu.SemaphoreType.DMA((n_chunk,)), pltpu.SemaphoreType.DMA, pltpu.SemaphoreType.DMA((n_chunk,)),
        pltpu.SemaphoreType.DMA((n_chunk,)), pltpu.SemaphoreType.DMA((n_chunk,)), pltpu.SemaphoreType.DMA((n_chunk,)),
        pltpu.SemaphoreType.DMA, pltpu.SemaphoreType.DMA, pltpu.SemaphoreType.DMA,
    ]
    d_z, gw_in, gw_gate, gw_out, gvec = pl.pallas_call(
        functools.partial(kernel, n_dev),
        out_shape=shapes,
        in_specs=[vmem] * 7,
        out_specs=[vmem] * 5,
        scratch_shapes=scratch,
        compiler_params=pltpu.CompilerParams(collective_id=0, has_side_effects=True, vmem_limit_bytes=66 * 1024 * 1000),
        name='triangle_backward',
    )(z_loc, dy_loc, mask_loc, w_in, w_gate, w_out, vecs)
    d_b_in = gvec[:4].reshape(4 * chan)
    return (d_z, gvec[5], gvec[6], gw_in, d_b_in, gvec[7], gvec[8], gw_out, gvec[9], gw_gate, gvec[4])


def solution(mesh):
    n_dev = mesh.shape['dap']
    pair_spec = P(('batch', 'dap'), None, None)
    mask_spec = P(('batch', 'dap'), None)
    vec_rep = P(None)
    mat_rep = P(None, None)
    vec_part = P('batch')
    mat_part = P('batch', None)
    in_specs = (pair_spec, mask_spec, pair_spec, vec_rep, vec_rep, mat_rep, vec_rep, vec_rep, vec_rep, mat_rep, vec_rep, mat_rep, vec_rep)
    out_specs = (pair_spec, vec_part, vec_part, mat_part, vec_part, vec_part, vec_part, mat_part, vec_part, mat_part, vec_part)
    return jax.shard_map(functools.partial(local_grads, n_dev), mesh=mesh, in_specs=in_specs, out_specs=out_specs, check_vma=False)
```

time: 872 us -> 423 us (0.49)
  waiting for transfers between devices: 485 us -> 0 us
  Pallas kernels: 0 us -> 405 us
  matrix products: 168 us -> 0 us
  local copies, waits for them, and re-layouts: 96.5 us -> 13.7 us
  blocking collectives: 48.9 us -> 0 us
  other arithmetic: 48.5 us -> 0.64 us
  between operations: 14.6 us -> 0.68 us
    pallas_call x0 -> x1, Pallas kernels: none -> 405 us  [local_grads(): pl.pallas_call(functools.partial(kernel, n_dev), out_shape=shapes, in_spe...]
    reduce_scatter x1 -> x0, waiting for transfers between devices: 312 us -> none  [local_grads(): d_act_b = lax.psum_scatter(d_b_part, 'dap', scatter_dimension=1, tiled=True)]
    all_gather x1 -> x0, waiting for transfers between devices: 174 us -> none  [local_grads(): b_full = lax.all_gather(act_b, 'dap', axis=1, tiled=True)]
    dot_general x12 -> x0, matrix products: 168 us -> none  [the longest x1 60.2 us: local_grads(): jnp.einsum('cij,cjk->cik', d_tri, b_full, preferred_element_type=jnp.floa...]
    dot_general x3 -> x0, local copies, waits for them, and re-layouts: 82.1 us -> none  [the longest x1 73 us: local_grads(): jnp.einsum('cij,cik->cjk', d_tri, act_a, preferred_element_type=jnp.float32)]
    psum x1 -> x0, blocking collectives: 48.9 us -> none  [local_grads(): lax.psum((d_in_scale, d_in_offset, d_w_in, d_b_in, d_out_scale, d_out_off...]
    reduce_sum x6 -> x0, other arithmetic: 19.7 us -> none  [the longest x2 7.1 us: norm_forward(): jnp.mean(centered * centered, axis=axis_id, keepdims=True) + LN_EPS]
    convert_element_type x11 -> x0, other arithmetic: 18.7 us -> none  [the longest x1 7.26 us: input_backward(): (dy_part.astype(jnp.float32) + norm_backward(d_znorm, in_hat, in_inv, ln_...]
  transfers between devices with their start and end apart: 2 -> 0, of which waited for: 2 -> 0; matrix products, arithmetic and copies ran while one was open for 11% -> 0% of each run, Pallas kernels for 0% -> 0%
where the time goes in v1:
time: 423 us; the launch traced here: 420 us
  Pallas kernels  405 us (96%)
  local copies, waits for them, and re-layouts  13.7 us (3%)
    pallas_call x1, Pallas kernels, local_grads(): pl.pallas_call(functools.partial(kernel, n_dev), out_shape=shapes, in_spe...  405 us
    unnamed x16, local copies, waits for them, and re-layouts  10.3 us

profile of v1, /device:TPU:21, one launch (start us, length us, event | category | flops | bytes accessed | tf_op | source)
XLA Modules:
  0.0 419.7 jit_solution(7002652488249779761)
XLA Ops:
  0.7 0.9 dynamic-update-slice
  1.5 0.8 dynamic-update-slice.1
  2.4 0.8 dynamic-update-slice.2
  3.2 0.8 dynamic-update-slice.3
  4.0 0.8 dynamic-update-slice.4
  4.9 0.8 dynamic-update-slice.5
  5.7 0.8 dynamic-update-slice.6
  6.5 0.6 pad_convert_fusion.par_ref
  7.2 404.7 %triangle_backward.1 = (bf16[24,384,128]{2,1,0:T(8,128)(2,1)}, bf16[128,512]{1,0:T(8,128)(2,1)}, bf16[128,128]{1,0:T(8,128)(2,1)}, bf16[128,128]{1,0:T(8,128)(2,1)}, bf16[16,128]{1,0:T(8,128)(2,1)}) custom-call(bf16[24,384,128]{2,1,0:T(8,128)(2,1)} %z_ref.1, bf16[24,384,128]{2,1,0:T(8,128)(2,1)} %dy_ref.1, s32[24,384]{1,0:T(8,128)} %mask_ref.1, ...), custom_call_target="tpu_custom_call" | custom-call | tf_op jit(solution)/shard_map/triangle_backward/pallas_call | solution.py:321
  411.9 1.2 slice_bitcast_fusion
  413.1 1.4 slice_bitcast_fusion.1
  414.5 0.0 copy-start
  414.5 0.0 copy-start.2
  414.5 0.0 copy-start.1
  414.5 3.3 copy.35
  417.8 0.0 copy-done
  417.8 0.7 copy.36
  418.5 0.0 copy-done.2
  418.5 0.6 copy.37
  419.1 0.0 copy-done.1
  419.1 0.6 copy.38
  (1 shorter events, 0.0 us)
Async XLA Ops:
  414.5 3.4 copy-start
  414.5 4.0 copy-start.2
  414.5 4.6 %copy-start.1 = (bf16[128,128]{1,0:T(8,128)(2,1)S(1)}, bf16[128,128]{1,0:T(8,128)(2,1)}, u32[]{:S(2)}) copy-start(bf16[128,128]{1,0:T(8,128)(2,1)} %get-tuple-element.47) | copy-start | bytes 98308

commit v2 on v1

v2 whole, which is shorter than its diff:
```python
import functools
import jax
import jax.numpy as jnp
from jax import lax
from jax.experimental import pallas as pl
from jax.experimental.pallas import tpu as pltpu
from jax.sharding import PartitionSpec as P

LN_EPS = 1e-5
CHUNK = 8
F32 = jnp.float32
BF16 = jnp.bfloat16


def mm(x_val, y_val):
    return lax.dot_general(x_val, y_val, (((1,), (0,)), ((), ())), preferred_element_type=F32)


def mm_nt(x_val, y_val):
    return lax.dot_general(x_val, y_val, (((1,), (1,)), ((), ())), preferred_element_type=F32)


def mm_tn(x_val, y_val):
    return lax.dot_general(x_val, y_val, (((0,), (0,)), ((), ())), preferred_element_type=F32)


def norm_stats(x_val):
    size = x_val.shape[0]
    mean_val = jnp.sum(x_val, axis=0, keepdims=True) * (1.0 / size)
    centered = x_val - mean_val
    inv_std = lax.rsqrt(jnp.sum(centered * centered, axis=0, keepdims=True) * (1.0 / size) + LN_EPS)
    return centered * inv_std, inv_std


def norm_back(grad_hat, x_hat, inv_std):
    size = x_hat.shape[0]
    mean_grad = jnp.sum(grad_hat, axis=0, keepdims=True) * (1.0 / size)
    mean_proj = jnp.sum(grad_hat * x_hat, axis=0, keepdims=True) * (1.0 / size)
    return inv_std * (grad_hat - mean_grad - x_hat * mean_proj)


def lane_fold(x_val):
    total = x_val[:, :128]
    for tile in range(1, x_val.shape[1] // 128):
        total = total + x_val[:, tile * 128:(tile + 1) * 128]
    return total


def kernel(n_dev, z_hbm, dy_hbm, mask_ref, w_in_ref, w_gate_ref, w_out_ref, *refs):
    par_refs = refs[:7]
    (dz_hbm, gmat_ref, gvec_ref,
     z_ref, dy_ref, dz_ref, w_in_t, w_gate_t, w_out_t, eye, par, cols,
     a_send, b_send, a_ch, b_ch, o_ch, o_row, do_send, do_ch, da_ch, da_row, db_ch, db_row,
     stage_a, stage_b, zn_keep, gg_keep, dzn_keep, m_acc, v_acc, v_row, m_recv, v_recv, g_send, g_all,
     z_sem, dy_sem, dz_sem, send_sem, a_sem, b_sem, o_sem, do_sem, da_sem, db_sem, m_sem, v_sem, g_sem) = refs[7:]
    rows, num, chan = z_ref.shape
    n_chunk = rows // CHUNK
    part = chan // n_dev
    tiles = num // 128
    me = lax.axis_index('dap')
    shard = g_send.shape[1]
    band = shard * n_dev

    barrier = pltpu.get_barrier_semaphore()

    def ring_peer(step):
        half = step // 2 + 1
        offset = half + lax.rem(step, 2) * (n_dev - 2 * half)
        return lax.rem(me + offset, n_dev)

    def hello(step, carry):
        pl.semaphore_signal(barrier, inc=1, device_id={'dap': ring_peer(step)}, device_id_type=pl.DeviceIdType.MESH)
        return carry

    lax.fori_loop(0, n_dev - 1, hello, 0)

    def block(chunk):
        return pl.ds(chunk * CHUNK, CHUNK)

    def load_z(chunk):
        return pltpu.make_async_copy(z_hbm.at[block(chunk)], z_ref.at[block(chunk)], z_sem.at[chunk])

    def load_dy():
        return pltpu.make_async_copy(dy_hbm, dy_ref, dy_sem)

    def store_dz(chunk):
        return pltpu.make_async_copy(dz_ref.at[block(chunk)], dz_hbm.at[block(chunk)], dz_sem.at[chunk])

    for chunk in range(n_chunk):
        load_z(chunk).start()
    load_dy().start()

    row_id = lax.broadcasted_iota(jnp.int32, (chan, chan), 0)
    col_id = lax.broadcasted_iota(jnp.int32, (chan, chan), 1)
    eye[...] = jnp.where(row_id == col_id, 1.0, 0.0).astype(BF16)
    par[...] = jnp.zeros_like(par)
    top = 0
    for ref in par_refs:
        par[top:top + ref.shape[0], :] = ref[...].astype(F32)
        top += ref.shape[0]
    cols[...] = jnp.transpose(par[...])
    for blk in range(4):
        w_in_t[blk * chan:(blk + 1) * chan, :] = jnp.transpose(w_in_ref[:, blk * chan:(blk + 1) * chan].astype(F32)).astype(BF16)
    w_gate_t[...] = jnp.transpose(w_gate_ref[...].astype(F32)).astype(BF16)
    w_out_t[...] = jnp.transpose(w_out_ref[...].astype(F32)).astype(BF16)
    m_acc[...] = jnp.zeros_like(m_acc)
    v_acc[...] = jnp.zeros_like(v_acc)
    v_row[...] = jnp.zeros_like(v_row)

    def col(idx):
        return cols[:, idx:idx + 1]

    def exchange(src_of, dst_ref, send_idx, recv_sem):
        def one(step, carry):
            peer = ring_peer(step)
            pltpu.make_async_remote_copy(
                src_ref=src_of(peer), dst_ref=dst_ref, send_sem=send_sem.at[send_idx], recv_sem=recv_sem,
                device_id={'dap': peer}, device_id_type=pl.DeviceIdType.MESH).start()
            return carry
        lax.fori_loop(0, n_dev - 1, one, 0)
        pltpu.make_async_copy(src_of(me), dst_ref, recv_sem).start()

    def take(ref, sem):
        pltpu.make_async_copy(ref, ref, sem).wait()

    def lanes(span, tile):
        return slice((span[0] + tile) * 128, (span[0] + tile + 1) * 128)

    def whole(span):
        return slice(span[0] * 128, span[1] * 128)

    def get_row(stage, row, span):
        return jnp.concatenate([stage[tile, pl.ds(row, chan, stride=CHUNK), :] for tile in range(*span)], axis=1)

    def put_row(stage, row, value, span):
        for tile in range(span[1] - span[0]):
            stage[span[0] + tile, pl.ds(row, chan, stride=CHUNK), :] = value[:, tile * 128:(tile + 1) * 128]

    def spread(stage, src, span):
        for tile in range(*span):
            stage[tile] = src[:, :, tile * 128:(tile + 1) * 128].astype(F32).reshape(chan * CHUNK, 128)

    def gather16(stage, dst, span):
        for tile in range(*span):
            dst[:, :, tile * 128:(tile + 1) * 128] = stage[tile].reshape(chan, CHUNK, 128).astype(BF16)

    everything = (0, tiles)

    def input_norm(row, span):
        z_t = mm_nt(eye[...], z_ref[row, whole(span), :])
        return norm_stats(z_t)

    def piece_of(blk, zn_t):
        return mm(w_in_t[blk * chan:(blk + 1) * chan, :], zn_t) + col(blk)

    def mask_of(row, span):
        return mask_ref[pl.ds(row, 1), :].astype(F32)[:, whole(span)]

    def input_piece(chunk, span):
        def one_row(r_in, carry_row):
            row = chunk * CHUNK + r_in
            in_hat, _ = input_norm(row, span)
            zn_t = (in_hat * col(5) + col(6)).astype(BF16)
            zn_keep[row, :, whole(span)] = zn_t
            mask_f = mask_of(row, span)
            put_row(stage_a, r_in, mask_f * jax.nn.sigmoid(piece_of(2, zn_t)) * piece_of(0, zn_t), span)
            put_row(stage_b, r_in, mask_f * jax.nn.sigmoid(piece_of(3, zn_t)) * piece_of(1, zn_t), span)
            return carry_row
        lax.fori_loop(0, CHUNK, one_row, 0)
        gather16(stage_b, b_send.at[chunk], span)
        gather16(stage_a, a_send.at[chunk], span)

    def input_send(chunk, span):
        exchange(lambda peer: b_send.at[chunk, pl.ds(peer * part, part), :, whole(span)],
                 b_ch.at[:, pl.ds(me * rows + chunk * CHUNK, CHUNK), whole(span)], 0, b_sem)
        exchange(lambda peer: a_send.at[chunk, pl.ds(peer * part, part), :, whole(span)],
                 a_ch.at[chunk, :, pl.ds(me * CHUNK, CHUNK), whole(span)], 1, a_sem.at[chunk])

    load_z(0).wait()
    for tile in range(tiles):
        input_piece(0, (tile, tile + 1))
        if tile == 0:
            pl.semaphore_wait(barrier, n_dev - 1)
        input_send(0, (tile, tile + 1))

    def input_chunk(chunk, carry):
        load_z(chunk).wait()
        input_piece(chunk, everything)
        input_send(chunk, everything)
        return carry

    lax.fori_loop(1, n_chunk, input_chunk, 0)

    take(b_ch, b_sem)

    def tri_chunk(chunk, carry):
        take(a_ch.at[chunk], a_sem.at[chunk])

        def one(idx, carry_ch):
            o_ch[chunk, idx] = mm_nt(a_ch[chunk, idx], b_ch[idx])
            return carry_ch
        lax.fori_loop(0, part, one, 0)
        exchange(lambda peer: o_ch.at[chunk, :, pl.ds(peer * CHUNK, CHUNK), :],
                 o_row.at[chunk, pl.ds(me * part, part)], 2, o_sem.at[chunk])
        return carry

    lax.fori_loop(0, n_chunk, tri_chunk, 0)
    load_dy().wait()

    def grow(blk, value):
        m_acc[blk * chan:(blk + 1) * chan, :] += value

    def chain_chunk(chunk, carry):
        take(o_row.at[chunk], o_sem.at[chunk])
        spread(stage_b, o_row.at[chunk], everything)

        def one_row(r_in, carry_row):
            row = chunk * CHUNK + r_in
            out_hat, out_inv = norm_stats(get_row(stage_b, r_in, everything))
            o_norm = (out_hat * col(7) + col(8)).astype(BF16)
            update = (mm(w_out_t[...], o_norm) + col(9)).astype(BF16).astype(F32)
            zn_t = zn_keep[row]
            sig_g = jax.nn.sigmoid(mm(w_gate_t[...], zn_t) + col(4))
            dy_t = mm_nt(eye[...], dy_ref[row])
            d_update = (sig_g * dy_t).astype(BF16)
            d_gate = dy_t * update * sig_g * (1.0 - sig_g)
            gate16 = d_gate.astype(BF16)
            gg_keep[row] = gate16
            v_acc[0] += lane_fold(d_gate)
            v_acc[1] += lane_fold(d_update.astype(F32))
            grow(0, mm_nt(zn_t, gate16))
            grow(1, mm_nt(o_norm, d_update))
            d_onorm = mm(w_out_ref[...], d_update).astype(BF16).astype(F32)
            v_acc[2] += lane_fold(d_onorm * out_hat)
            v_acc[3] += lane_fold(d_onorm)
            put_row(stage_a, r_in, norm_back(d_onorm * col(7), out_hat, out_inv), everything)
            return carry_row
        lax.fori_loop(0, CHUNK, one_row, 0)
        gather16(stage_a, do_send.at[chunk], everything)
        exchange(lambda peer: do_send.at[chunk, pl.ds(peer * part, part)],
                 do_ch.at[chunk, :, pl.ds(me * CHUNK, CHUNK), :], 3, do_sem.at[chunk])
        return carry

    lax.fori_loop(0, n_chunk, chain_chunk, 0)

    def share_out(turn, kinds):
        for pos, kind in enumerate(kinds):
            v_row[turn, pos:pos + 1, :] = jnp.sum(jnp.transpose(v_acc[kind]), axis=0, keepdims=True)
        exchange(lambda peer: m_acc.at[pl.ds(turn * band + peer * shard, shard)], m_recv.at[turn, me], 6, m_sem.at[turn])
        exchange(lambda peer: v_row.at[turn], v_recv.at[turn, me], 7, v_sem.at[turn])

    def share_sum(turn):
        take(m_recv.at[turn], m_sem.at[turn])
        g_send[turn] = jnp.sum(m_recv[turn], axis=0).astype(BF16)
        exchange(lambda peer: g_send.at[turn], g_all.at[pl.ds(turn * band + me * shard, shard)], 8, g_sem)
        take(v_recv.at[turn], v_sem.at[turn])
        gvec_ref[turn] = jnp.sum(v_recv[turn], axis=0).astype(BF16)

    share_out(0, (0, 1, 2, 3))

    def da_chunk(chunk, carry):
        take(do_ch.at[chunk], do_sem.at[chunk])

        def one(idx, carry_ch):
            da_ch[chunk, idx] = mm(do_ch[chunk, idx], b_ch[idx]).astype(BF16)
            return carry_ch
        lax.fori_loop(0, part, one, 0)
        exchange(lambda peer: da_ch.at[chunk, :, pl.ds(peer * CHUNK, CHUNK), :],
                 da_row.at[chunk, pl.ds(me * part, part)], 4, da_sem.at[chunk])
        return carry

    lax.fori_loop(0, n_chunk, da_chunk, 0)

    def db_one(idx, carry):
        total = mm_tn(do_ch[0, idx], a_ch[0, idx])
        for chunk in range(1, n_chunk):
            total += mm_tn(do_ch[chunk, idx], a_ch[chunk, idx])
        db_ch[idx] = total.astype(BF16)
        return carry

    lax.fori_loop(0, part, db_one, 0)

    def db_send(chunk, span, sem):
        exchange(lambda peer: db_ch.at[:, pl.ds(peer * rows + chunk * CHUNK, CHUNK), whole(span)],
                 db_row.at[chunk, pl.ds(me * part, part), :, whole(span)], 5, sem)

    last = n_chunk - 1
    for chunk in range(last):
        db_send(chunk, everything, db_sem.at[chunk])
    for tile in range(tiles):
        db_send(last, (tile, tile + 1), db_sem.at[last + tile])
    share_sum(0)

    def half_back(row, r_in, stage, blk, zn_t, span):
        grad = get_row(stage, r_in, span) * mask_of(row, span)
        proj = piece_of(blk, zn_t)
        sig = jax.nn.sigmoid(piece_of(blk + 2, zn_t))
        d_proj = grad * sig
        d_sig = d_proj * proj * (1.0 - sig)
        grow(2 + 2 * blk, mm_nt(zn_t, d_proj.astype(BF16)))
        grow(3 + 2 * blk, mm_nt(zn_t, d_sig.astype(BF16)))
        v_acc[4 + 2 * blk] += lane_fold(d_proj)
        v_acc[5 + 2 * blk] += lane_fold(d_sig)
        return (mm(w_in_ref[:, blk * chan:(blk + 1) * chan], d_proj.astype(BF16))
                + mm(w_in_ref[:, (blk + 2) * chan:(blk + 3) * chan], d_sig.astype(BF16)))

    def early_chunk(chunk, carry):
        take(da_row.at[chunk], da_sem.at[chunk])
        spread(stage_a, da_row.at[chunk], everything)

        def one_row(r_in, carry_row):
            row = chunk * CHUNK + r_in
            dzn_keep[row] = mm(w_gate_ref[...], gg_keep[row]) + half_back(row, r_in, stage_a, 0, zn_keep[row], everything)
            return carry_row
        lax.fori_loop(0, CHUNK, one_row, 0)
        return carry

    lax.fori_loop(0, n_chunk, early_chunk, 0)
    share_out(1, (4, 5))

    def late_piece(chunk, span):
        spread(stage_b, db_row.at[chunk], span)

        def one_row(r_in, carry_row):
            row = chunk * CHUNK + r_in
            zn_t = zn_keep[row, :, whole(span)]
            d_znorm = (dzn_keep[row, :, whole(span)] + half_back(row, r_in, stage_b, 1, zn_t, span)).astype(BF16).astype(F32)
            in_hat, in_inv = input_norm(row, span)
            v_acc[8] += lane_fold(d_znorm * in_hat)
            v_acc[9] += lane_fold(d_znorm)
            dz_t = mm_nt(eye[...], dy_ref[row, whole(span), :]) + norm_back(d_znorm * col(5), in_hat, in_inv)
            dz_ref[row, whole(span), :] = jnp.transpose(dz_t).astype(BF16)
            return carry_row
        lax.fori_loop(0, CHUNK, one_row, 0)

    def late_chunk(chunk, carry):
        take(db_row.at[chunk], db_sem.at[chunk])
        late_piece(chunk, everything)
        store_dz(chunk).start()
        return carry

    lax.fori_loop(0, last, late_chunk, 0)
    for tile in range(tiles):
        span = (tile, tile + 1)
        take(db_row.at[last, :, :, whole(span)], db_sem.at[last + tile])
        late_piece(last, span)
    share_out(2, (6, 7, 8, 9))
    store_dz(last).start()
    share_sum(1)
    share_sum(2)
    take(g_all, g_sem)
    for pos, blk in enumerate((4, 5, 0, 2, 1, 3)):
        gmat_ref[:, blk * chan:(blk + 1) * chan] = g_all[pos * chan:(pos + 1) * chan, :]

    others = (n_dev - 1) * part
    for sent, ref in ((0, b_send), (1, a_send), (3, do_send), (2, o_row), (4, da_row), (5, db_row)):
        take(ref.at[:, pl.ds(0, others)], send_sem.at[sent])
    take(m_recv.at[:, pl.ds(0, n_dev - 1)], send_sem.at[6])
    take(v_recv.at[:, pl.ds(0, n_dev - 1)], send_sem.at[7])
    take(g_all.at[pl.ds(0, 3 * (n_dev - 1) * shard)], send_sem.at[8])
    for chunk in range(n_chunk):
        store_dz(chunk).wait()


def local_grads(n_dev, z_loc, mask_loc, dy_loc, ln_in_scale, ln_in_offset, w_in, b_in, ln_out_scale, ln_out_offset, w_out, b_out, w_gate, b_gate):
    rows, num, chan = z_loc.shape
    n_chunk = rows // CHUNK
    part = chan // n_dev
    tiles = num // 128
    shard = 2 * chan // n_dev
    params = [vec.reshape(-1, chan) for vec in (b_in, b_gate, ln_in_scale, ln_in_offset, ln_out_scale, ln_out_offset, b_out)]
    vmem = pl.BlockSpec(memory_space=pltpu.VMEM)
    hbm = pl.BlockSpec(memory_space=pl.ANY)
    shapes = [jax.ShapeDtypeStruct((rows, num, chan), BF16), jax.ShapeDtypeStruct((chan, 6 * chan), BF16), jax.ShapeDtypeStruct((3, 8, chan), BF16)]
    pair = pltpu.VMEM((rows, num, chan), BF16)
    by_row = pltpu.VMEM((n_chunk, chan, CHUNK, num), BF16)
    by_chan = pltpu.VMEM((n_chunk, part, n_dev * CHUNK, num), BF16)
    by_chan_all = pltpu.VMEM((part, num, num), BF16)
    stage = pltpu.VMEM((tiles, chan * CHUNK, 128), F32)
    keep = pltpu.VMEM((rows, chan, num), BF16)
    square = pltpu.VMEM((chan, chan), BF16)
    dma = pltpu.SemaphoreType.DMA
    scratch = [
        pair, pair, pair, pltpu.VMEM((4 * chan, chan), BF16), square, square, square,
        pltpu.VMEM((chan, chan), F32), pltpu.VMEM((chan, chan), F32),
        by_row, by_row, by_chan, by_chan_all,
        pltpu.VMEM((n_chunk, part, n_dev * CHUNK, num), F32), pltpu.VMEM((n_chunk, chan, CHUNK, num), F32),
        by_row, by_chan, by_chan, by_row, by_chan_all, by_row,
        stage, stage, keep, keep, pltpu.VMEM((rows, chan, num), F32),
        pltpu.VMEM((6 * chan, chan), F32), pltpu.VMEM((10, chan, chan), F32), pltpu.VMEM((3, 8, chan), F32),
        pltpu.VMEM((3, n_dev, shard, chan), F32), pltpu.VMEM((3, n_dev, 8, chan), F32),
        pltpu.VMEM((3, shard, chan), BF16), pltpu.VMEM((6 * chan, chan), BF16),
        dma((n_chunk,)), dma, dma((n_chunk,)), dma((9,)),
        dma((n_chunk,)), dma, dma((n_chunk,)), dma((n_chunk,)), dma((n_chunk,)), dma((n_chunk - 1 + tiles,)),
        dma((3,)), dma((3,)), dma,
    ]
    d_z, gmat, gvec = pl.pallas_call(
        functools.partial(kernel, n_dev),
        out_shape=shapes,
        in_specs=[hbm, hbm] + [vmem] * 11,
        out_specs=[hbm, vmem, vmem],
        scratch_shapes=scratch,
        compiler_params=pltpu.CompilerParams(collective_id=0, has_side_effects=True, vmem_limit_bytes=67000000),
        name='triangle_backward',
    )(z_loc, dy_loc, mask_loc, w_in, w_gate, w_out, *params)
    d_b_in = jnp.concatenate([gvec[1, 0], gvec[2, 0], gvec[1, 1], gvec[2, 1]])
    return (d_z, gvec[2, 2], gvec[2, 3], gmat[:, :4 * chan], d_b_in, gvec[0, 2], gvec[0, 3],
            gmat[:, 5 * chan:], gvec[0, 1], gmat[:, 4 * chan:5 * chan], gvec[0, 0])


def solution(mesh):
    n_dev = mesh.shape['dap']
    pair_spec = P(('batch', 'dap'), None, None)
    mask_spec = P(('batch', 'dap'), None)
    vec_rep = P(None)
    mat_rep = P(None, None)
    vec_part = P('batch')
    mat_part = P('batch', None)
    in_specs = (pair_spec, mask_spec, pair_spec, vec_rep, vec_rep, mat_rep, vec_rep, vec_rep, vec_rep, mat_rep, vec_rep, mat_rep, vec_rep)
    out_specs = (pair_spec, vec_part, vec_part, mat_part, vec_part, vec_part, vec_part, mat_part, vec_part, mat_part, vec_part)
    return jax.shard_map(functools.partial(local_grads, n_dev), mesh=mesh, in_specs=in_specs, out_specs=out_specs, check_vma=False)
```

time: 423 us -> 410 us (0.969)
  local copies, waits for them, and re-layouts: 13.7 us -> 7.64 us
    unnamed x16 -> x1, local copies, waits for them, and re-layouts: 10.3 us -> 3.3 us
where the time goes in v2:
time: 410 us
  Pallas kernels  401 us (98%)
  local copies, waits for them, and re-layouts  7.64 us (2%)
    pallas_call x1, Pallas kernels, local_grads(): pl.pallas_call(functools.partial(kernel, n_dev), out_shape=shapes, in_spe...  401 us

profile of v2, /device:TPU:21, one launch (start us, length us, event | category | flops | bytes accessed | tf_op | source)
XLA Modules:
  0.0 409.6 jit_solution(1310899143786910718)
XLA Ops:
  0.6 400.8 %triangle_backward.1 = (bf16[24,384,128]{2,1,0:T(8,128)(2,1)}, bf16[128,768]{1,0:T(8,128)(2,1)}, bf16[3,8,128]{2,1,0:T(8,128)(2,1)}) custom-call(bf16[24,384,128]{2,1,0:T(8,128)(2,1)} %z_hbm.1, bf16[24,384,128]{2,1,0:T(8,128)(2,1)} %dy_hbm.1, s32[24,384]{1,0:T(8,128)} %mask_ref.1, bf16[128,512]{1,0:T(8,128)(2,1)} %w_in_ref.1, bf16[128,128]{1,0:T(8,128)(2,1)} %w_gate_ref.1, ...), custom_call_target="tpu_custom_call" | custom-call | tf_op jit(solution)/shard_map/triangle_backward/pallas_call | solution.py:397
  401.4 1.4 slice_bitcast_fusion
  402.8 0.6 pad_maximum_fusion
  403.4 1.4 fusion
  404.8 1.6 slice.41
  406.4 3.3 copy.25

commit v3 on v2

--- a/solution.py
+++ b/solution.py
@@ -244,19 +244,21 @@
     lax.fori_loop(0, n_chunk, chain_chunk, 0)
 
     def share_out(turn, kinds):
-        for pos, kind in enumerate(kinds):
-            v_row[turn, pos:pos + 1, :] = jnp.sum(jnp.transpose(v_acc[kind]), axis=0, keepdims=True)
         exchange(lambda peer: m_acc.at[pl.ds(turn * band + peer * shard, shard)], m_recv.at[turn, me], 6, m_sem.at[turn])
-        exchange(lambda peer: v_row.at[turn], v_recv.at[turn, me], 7, v_sem.at[turn])
+        if kinds:
+            for pos, kind in enumerate(kinds):
+                v_row[turn - 1, pos:pos + 1, :] = jnp.sum(jnp.transpose(v_acc[kind]), axis=0, keepdims=True)
+            exchange(lambda peer: v_row.at[turn - 1], v_recv.at[turn - 1, me], 7, v_sem.at[turn - 1])
 
     def share_sum(turn):
         take(m_recv.at[turn], m_sem.at[turn])
         g_send[turn] = jnp.sum(m_recv[turn], axis=0).astype(BF16)
         exchange(lambda peer: g_send.at[turn], g_all.at[pl.ds(turn * band + me * shard, shard)], 8, g_sem)
-        take(v_recv.at[turn], v_sem.at[turn])
-        gvec_ref[turn] = jnp.sum(v_recv[turn], axis=0).astype(BF16)
-
-    share_out(0, (0, 1, 2, 3))
+        if turn:
+            take(v_recv.at[turn - 1], v_sem.at[turn - 1])
+            gvec_ref[turn - 1] = jnp.sum(v_recv[turn - 1], axis=0).astype(BF16)
+
+    share_out(0, ())
 
     def da_chunk(chunk, carry):
         take(do_ch.at[chunk], do_sem.at[chunk])
@@ -316,7 +318,7 @@
         return carry
 
     lax.fori_loop(0, n_chunk, early_chunk, 0)
-    share_out(1, (4, 5))
+    share_out(1, (0, 1, 2, 3, 4, 5))
 
     def late_piece(chunk, span):
         spread(stage_b, db_row.at[chunk], span)
@@ -362,6 +364,41 @@
         store_dz(chunk).wait()
 
 
+def finish(dz_in, gmat_ref, gvec_ref, dz_out, gw_in_ref, gw_gate_ref, gw_out_ref, b_in_ref, b_gate_ref, in_scale_ref, in_offset_ref,
+           out_scale_ref, out_offset_ref, b_out_ref, hold, in_sem, out_sem):
+    rows, _, chan = hold.shape
+    n_chunk = rows // CHUNK
+
+    def pull(chunk):
+        span = pl.ds(chunk * CHUNK, CHUNK)
+        return pltpu.make_async_copy(dz_in.at[span], hold.at[span], in_sem.at[chunk])
+
+    def push(chunk):
+        span = pl.ds(chunk * CHUNK, CHUNK)
+        return pltpu.make_async_copy(hold.at[span], dz_out.at[span], out_sem.at[chunk])
+
+    for chunk in range(n_chunk):
+        pull(chunk).start()
+    gw_in_ref[...] = gmat_ref[:, :4 * chan]
+    gw_gate_ref[...] = gmat_ref[:, 4 * chan:5 * chan]
+    gw_out_ref[...] = gmat_ref[:, 5 * chan:]
+    b_gate_ref[...] = gvec_ref[0, 0:1, :]
+    b_out_ref[...] = gvec_ref[0, 1:2, :]
+    out_scale_ref[...] = gvec_ref[0, 2:3, :]
+    out_offset_ref[...] = gvec_ref[0, 3:4, :]
+    b_in_ref[0:1, :] = gvec_ref[0, 4:5, :]
+    b_in_ref[2:3, :] = gvec_ref[0, 5:6, :]
+    b_in_ref[1:2, :] = gvec_ref[1, 0:1, :]
+    b_in_ref[3:4, :] = gvec_ref[1, 1:2, :]
+    in_scale_ref[...] = gvec_ref[1, 2:3, :]
+    in_offset_ref[...] = gvec_ref[1, 3:4, :]
+    for chunk in range(n_chunk):
+        pull(chunk).wait()
+        push(chunk).start()
+    for chunk in range(n_chunk):
+        push(chunk).wait()
+
+
 def local_grads(n_dev, z_loc, mask_loc, dy_loc, ln_in_scale, ln_in_offset, w_in, b_in, ln_out_scale, ln_out_offset, w_out, b_out, w_gate, b_gate):
     rows, num, chan = z_loc.shape
     n_chunk = rows // CHUNK
@@ -371,7 +408,7 @@
     params = [vec.reshape(-1, chan) for vec in (b_in, b_gate, ln_in_scale, ln_in_offset, ln_out_scale, ln_out_offset, b_out)]
     vmem = pl.BlockSpec(memory_space=pltpu.VMEM)
     hbm = pl.BlockSpec(memory_space=pl.ANY)
-    shapes = [jax.ShapeDtypeStruct((rows, num, chan), BF16), jax.ShapeDtypeStruct((chan, 6 * chan), BF16), jax.ShapeDtypeStruct((3, 8, chan), BF16)]
+    shapes = [jax.ShapeDtypeStruct((rows, num, chan), BF16), jax.ShapeDtypeStruct((chan, 6 * chan), BF16), jax.ShapeDtypeStruct((2, 8, chan), BF16)]
     pair = pltpu.VMEM((rows, num, chan), BF16)
     by_row = pltpu.VMEM((n_chunk, chan, CHUNK, num), BF16)
     by_chan = pltpu.VMEM((n_chunk, part, n_dev * CHUNK, num), BF16)
@@ -387,12 +424,12 @@
         pltpu.VMEM((n_chunk, part, n_dev * CHUNK, num), F32), pltpu.VMEM((n_chunk, chan, CHUNK, num), F32),
         by_row, by_chan, by_chan, by_row, by_chan_all, by_row,
         stage, stage, keep, keep, pltpu.VMEM((rows, chan, num), F32),
-        pltpu.VMEM((6 * chan, chan), F32), pltpu.VMEM((10, chan, chan), F32), pltpu.VMEM((3, 8, chan), F32),
-        pltpu.VMEM((3, n_dev, shard, chan), F32), pltpu.VMEM((3, n_dev, 8, chan), F32),
+        pltpu.VMEM((6 * chan, chan), F32), pltpu.VMEM((10, chan, chan), F32), pltpu.VMEM((2, 8, chan), F32),
+        pltpu.VMEM((3, n_dev, shard, chan), F32), pltpu.VMEM((2, n_dev, 8, chan), F32),
         pltpu.VMEM((3, shard, chan), BF16), pltpu.VMEM((6 * chan, chan), BF16),
         dma((n_chunk,)), dma, dma((n_chunk,)), dma((9,)),
         dma((n_chunk,)), dma, dma((n_chunk,)), dma((n_chunk,)), dma((n_chunk,)), dma((n_chunk - 1 + tiles,)),
-        dma((3,)), dma((3,)), dma,
+        dma((3,)), dma((2,)), dma,
     ]
     d_z, gmat, gvec = pl.pallas_call(
         functools.partial(kernel, n_dev),
@@ -403,9 +440,19 @@
         compiler_params=pltpu.CompilerParams(collective_id=0, has_side_effects=True, vmem_limit_bytes=67000000),
         name='triangle_backward',
     )(z_loc, dy_loc, mask_loc, w_in, w_gate, w_out, *params)
-    d_b_in = jnp.concatenate([gvec[1, 0], gvec[2, 0], gvec[1, 1], gvec[2, 1]])
-    return (d_z, gvec[2, 2], gvec[2, 3], gmat[:, :4 * chan], d_b_in, gvec[0, 2], gvec[0, 3],
-            gmat[:, 5 * chan:], gvec[0, 1], gmat[:, 4 * chan:5 * chan], gvec[0, 0])
+    row = jax.ShapeDtypeStruct((1, chan), BF16)
+    square_out = jax.ShapeDtypeStruct((chan, chan), BF16)
+    outs = pl.pallas_call(
+        finish,
+        out_shape=[shapes[0], jax.ShapeDtypeStruct((chan, 4 * chan), BF16), square_out, square_out, jax.ShapeDtypeStruct((4, chan), BF16)] + [row] * 6,
+        in_specs=[hbm, vmem, vmem],
+        out_specs=[hbm] + [vmem] * 10,
+        scratch_shapes=[pair, dma((n_chunk,)), dma((n_chunk,))],
+        name='write_outputs',
+    )(d_z, gmat, gvec)
+    d_z, gw_in, gw_gate, gw_out = outs[:4]
+    d_b_in, d_b_gate, d_in_scale, d_in_offset, d_out_scale, d_out_offset, d_b_out = [vec.reshape(-1) for vec in outs[4:]]
+    return (d_z, d_in_scale, d_in_offset, gw_in, d_b_in, d_out_scale, d_out_offset, gw_out, d_b_out, gw_gate, d_b_gate)
 
 
 def solution(mesh):

time: 410 us -> 405 us (0.988)
  local copies, waits for them, and re-layouts: 7.64 us -> 0 us
    pallas_call x1, Pallas kernels: 401 us -> 396 us  [local_grads(): pl.pallas_call(functools.partial(kernel, n_dev), out_shape=shapes, in_spe...]
    pallas_call x0 -> x1, Pallas kernels: none -> 4.2 us  [local_grads(): pl.pallas_call(finish, out_shape=[shapes[0], jax.ShapeDtypeStruct((chan,...]
where the time goes in v3:
time: 405 us; the launch traced here: 401 us
  Pallas kernels  401 us (99%)
    pallas_call x1, Pallas kernels, local_grads(): pl.pallas_call(functools.partial(kernel, n_dev), out_shape=shapes, in_spe...  396 us

profile of v3, /device:TPU:21, one launch (start us, length us, event | category | flops | bytes accessed | tf_op | source)
XLA Modules:
  0.0 401.2 jit_solution(15835979299230945433)
XLA Ops:
  0.6 396.3 %triangle_backward.1 = (bf16[24,384,128]{2,1,0:T(8,128)(2,1)}, bf16[128,768]{1,0:T(8,128)(2,1)}, bf16[2,8,128]{2,1,0:T(8,128)(2,1)}) custom-call(bf16[24,384,128]{2,1,0:T(8,128)(2,1)} %z_hbm.1, bf16[24,384,128]{2,1,0:T(8,128)(2,1)} %dy_hbm.1, s32[24,384]{1,0:T(8,128)} %mask_ref.1, bf16[128,512]{1,0:T(8,128)(2,1)} %w_in_ref.1, bf16[128,128]{1,0:T(8,128)(2,1)} %w_gate_ref.1, ...), custom_call_target="tpu_custom_call" | custom-call | tf_op jit(solution)/shard_map/triangle_backward/pallas_call | solution.py:434
  397.0 4.2 %write_outputs.1 = (bf16[24,384,128]{2,1,0:T(8,128)(2,1)}, bf16[128,512]{1,0:T(8,128)(2,1)}, bf16[128,128]{1,0:T(8,128)(2,1)}, bf16[128,128]{1,0:T(8,128)(2,1)},...) custom-call(bf16[24,384,128]{2,1,0:T(8,128)(2,1)} %get-tuple-element, ...), custom_call_target="tpu_custom_call" | custom-call | tf_op jit(solution)/shard_map/write_outputs/pallas_call | solution.py:445
